TPU v7x, 256 devices: a whole 4x4x8 slice. The times are simulated.
256 devices in a mesh: gx: 16 (over z, x_lo), gy: 16 (over y, x_hi, core).
Axes of the slice: x: 4 (x_hi: 2, x_lo: 2; x = x_hi * 2 + x_lo), y: 4, z: 8, core: 2. Of those that a mesh axis runs over, the one named last changes fastest.
Arguments:
- gradient: float32 [2048, 512], P('gx', 'gy'), may hold values from -6 to 6
- stat_old: float32 [2048, 2048], P('gx', 'gy'), may hold values from -1.001 to 1.001, as said below
Outputs:
- statistic: float32 [2048, 2048], P('gx', 'gy')
- inverse_root: float32 [2048, 2048], P('gx', 'gy')
Inputs may be any that keep to these rules, and one draw needn't show every extreme that they name: stat_old is symmetric positive semidefinite with unit diagonal, the Gram matrix of 2048 unit-length rows of 512 entries.
All inputs are finite; a program needn't handle non-finite values.
Results may differ from a plain program's by a relative error of at most 0.0003.
Values sent between devices are 32-bit elements.
A program may use at most 64 MiB of HBM per device.

v0:
```python
import jax
import jax.numpy as jnp
from jax import lax
from jax.sharding import Mesh
from jax.sharding import PartitionSpec as P

GY = ("gy_0", "gy_1", "gy_2")
GX = ("gx_0", "gx_1")
GX_GY = ("gx_0", "gx_1", "gy_0", "gy_1", "gy_2")


def gather_axes(array, axes, dim):
    filled = array
    for number in range(len(axes) - 1, -1, -1):
        filled = lax.all_gather(filled, axes[number], axis=dim, tiled=True)
    return filled


def folded(array, axes, dim, take_in, carry):
    everything = jax.tree.map(lambda part: gather_axes(part, axes, dim), array)
    return take_in(carry, everything, jnp.int32(0))


def spread(array, axes, root):
    array = jnp.where(lax.axis_index(axes) == root, array, jnp.zeros_like(array))
    for axis in axes:
        array = lax.psum(array, axis)
    return array


def over_axes(array, axes):
    for axis in axes:
        array = lax.psum(array, axis)
    return array


def matmul(leading, trailing):
    return jnp.dot(
        leading, trailing, preferred_element_type=jnp.float32, precision=lax.Precision.HIGHEST
    )


def panels(factor_one, factor_two):
    whole_row = lax.all_gather(factor_one, GY, axis=1, tiled=True)

    def accumulate(running, shard_rows, first_row):
        matching = lax.dynamic_slice_in_dim(whole_row, first_row, shard_rows.shape[0], 1)
        return running + matmul(matching, shard_rows)

    empty = jnp.zeros((factor_one.shape[0], factor_two.shape[1]), jnp.float32)
    return folded(factor_two, GX, 0, accumulate, empty)


def product(factor_one, factor_two):
    return panels(factor_one, factor_two)


def local(gradient, stat_old):
    count_rows = lax.axis_size(GX)
    count_cols = lax.axis_size(GY)
    factor = count_rows // count_cols
    piece_width = stat_old.shape[0]
    row_index = lax.axis_index(GX)
    col_index = lax.axis_index(GY)
    panel_rows = lax.all_gather(gradient, GY, axis=1, tiled=True)
    outer_parts = []
    for member in range(factor):
        column_rows = spread(panel_rows, GX, col_index * factor + member)
        outer_parts.append(matmul(panel_rows, column_rows.T))
    outer = jnp.concatenate(outer_parts, axis=1) / panel_rows.shape[1]
    statistic = 0.9 * stat_old + outer
    squares = over_axes(jnp.sum(statistic * statistic), GX_GY)
    divisor = 2.0 * jnp.sqrt(squares / (piece_width * count_rows))
    global_rows = row_index * piece_width + lax.broadcasted_iota(jnp.int32, stat_old.shape, 0)
    global_cols = col_index * (factor * piece_width) + lax.broadcasted_iota(
        jnp.int32, stat_old.shape, 1
    )
    identity = (global_rows == global_cols).astype(jnp.float32)
    normed = statistic / divisor
    first_step = 1.5 * identity - 0.5 * normed
    root_half = product(normed, first_step)
    product_mid = product(first_step, root_half)
    second_step = 1.5 * identity - 0.5 * product_mid
    inverse_root = product(second_step, first_step)
    return (statistic, inverse_root)


def solution(mesh):
    torus = Mesh(mesh.devices.reshape(8, 2, 4, 2, 2), ("gx_0", "gx_1", "gy_0", "gy_1", "gy_2"))
    placed = (P(GX, GY), P(GX, GY))
    return jax.shard_map(
        local, mesh=torus, in_specs=placed, out_specs=(P(GX, GY), P(GX, GY)), check_vma=False
    )
```

profile of v0, /device:TPU:1, one launch (start us, length us, event | category | flops | bytes accessed | tf_op | source)
XLA Modules:
  0.0 436.5 jit_solution(8363940582427046131)
XLA Ops:
  7.2 0.0 all-reduce.3.cloned.1.call-start
  7.2 0.7 copy-done.3
  7.9 26.8 %all_gather.26 = f32[128,512]{0,1:T(8,128)S(1)} all-gather(f32[128,32]{0,1:T(8,128)S(1)} %copy-done.3), channel_id=1, replica_groups=mesh['gx_0'=8,'gx_1'=2,'gy_0'=4,'gy_1'=2,'gy_2'=2] {'gy_0','gy_1','gy_2'}, dimensions={1}, use_global_device_ids=true | all-gather | bytes 278528 | tf_op jit(solution)/shard_map/all_gather | solution.py:65
  34.7 0.7 broadcast_select_fusion
  35.4 0.0 all-reduce.5.cloned.1.call-start
  35.4 65.4 %all-reduce.3.cloned.1.call-done = f32[128,512]{0,1:T(8,128)} async-done(((f32[128,512]{0,1:T(8,128)}), f32[128,512]{0,1:T(8,128)}) %all-reduce.3.cloned.1.call-update) | async-done | bytes 262160 | tf_op jit(solution)/shard_map/psum | solution.py:27
  100.9 0.0 all-gather.10.cloned.1.call-start
  100.9 0.8 copy-done.2
  101.7 0.1 copy.4
  101.8 39.7 %all-reduce.5.cloned.1.call-done = f32[128,512]{0,1:T(8,128)} async-done(((f32[128,512]{0,1:T(8,128)}), f32[128,512]{0,1:T(8,128)}) %all-reduce.5.cloned.1.call-update) | async-done | bytes 262160 | tf_op jit(solution)/shard_map/psum | solution.py:27
  141.4 2.1 multiply_reduce_fusion
  143.6 14.5 %psum.51 = f32[]{:T(128)} all-reduce(f32[]{:T(128)} %get-tuple-element.6), channel_id=1, replica_groups=mesh['gx_0'=8,'gx_1'=2,'gy_0'=4,'gy_1'=2,'gy_2'=2] {'gx_0'}, use_global_device_ids=true, to_apply=%region_3.4 | all-reduce | flops 1 | bytes 8 | tf_op jit(solution)/shard_map/psum | solution.py:33
  158.0 4.4 %psum.52 = f32[]{:T(128)} all-reduce(f32[]{:T(128)} %psum.51), channel_id=1, replica_groups=mesh['gx_0'=8,'gx_1'=2,'gy_0'=4,'gy_1'=2,'gy_2'=2] {'gx_1'}, use_global_device_ids=true, to_apply=%region_4.5 | all-reduce | flops 1 | bytes 8 | tf_op jit(solution)/shard_map/psum | solution.py:33
  162.4 9.1 %psum.53 = f32[]{:T(128)} all-reduce(f32[]{:T(128)} %psum.52), channel_id=1, replica_groups=mesh['gx_0'=8,'gx_1'=2,'gy_0'=4,'gy_1'=2,'gy_2'=2] {'gy_0'}, use_global_device_ids=true, to_apply=%region_5.6 | all-reduce | flops 1 | bytes 8 | tf_op jit(solution)/shard_map/psum | solution.py:33
  171.5 5.9 %psum.54 = f32[]{:T(128)} all-reduce(f32[]{:T(128)} %psum.53), channel_id=1, replica_groups=mesh['gx_0'=8,'gx_1'=2,'gy_0'=4,'gy_1'=2,'gy_2'=2] {'gy_1'}, use_global_device_ids=true, to_apply=%region_6.7 | all-reduce | flops 1 | bytes 8 | tf_op jit(solution)/shard_map/psum | solution.py:33
  177.4 11.8 %psum.55 = f32[]{:T(128)} all-reduce(f32[]{:T(128)} %psum.54), channel_id=1, replica_groups=mesh['gx_0'=8,'gx_1'=2,'gy_0'=4,'gy_1'=2,'gy_2'=2] {'gy_2'}, use_global_device_ids=true, to_apply=%region_7.8 | all-reduce | flops 1 | bytes 8 | tf_op jit(solution)/shard_map/psum | solution.py:33
  189.9 0.6 select_subtract_fusion
  190.5 3.9 all_gather.29
  194.4 0.0 all-gather.8.cloned.1.call-start
  194.5 0.5 all-gather.8.cloned.1.call-update
  195.0 0.5 all-gather.6.cloned.1.call-update
  195.6 29.4 %all-gather.10.cloned.1.call-done = f32[2048,128]{0,1:T(8,128)} async-done(((f32[256,128]{0,1:T(8,128)}), f32[2048,128]{0,1:T(8,128)}) %all-gather.10.cloned.1.call-update) | async-done | bytes 1048592 | tf_op jit(solution)/shard_map/all_gather | solution.py:15
  225.0 57.2 %all-gather.8.cloned.1.call-done = f32[128,2048]{0,1:T(8,128)} async-done(((f32[128,128]{0,1:T(8,128)}), f32[128,2048]{0,1:T(8,128)}) %all-gather.8.cloned.1.call-update) | async-done | bytes 1048592 | tf_op jit(solution)/shard_map/all_gather | solution.py:44
  282.2 3.4 fusion.3
  285.6 3.9 all_gather.31
  289.5 0.0 all-gather.14.cloned.1.call-start
  289.6 44.7 %all-gather.6.cloned.1.call-done = f32[128,2048]{0,1:T(8,128)} async-done(((f32[128,128]{0,1:T(8,128)}), f32[128,2048]{0,1:T(8,128)}) %all-gather.6.cloned.1.call-update) | async-done | bytes 1048592 | tf_op jit(solution)/shard_map/all_gather | solution.py:44
  334.2 33.6 %all-gather.12.cloned.1.call-done = f32[2048,128]{1,0:T(8,128)} async-done(((f32[256,128]{1,0:T(8,128)}), f32[2048,128]{1,0:T(8,128)}) %all-gather.12.cloned.1.call-update) | async-done | bytes 1048592 | tf_op jit(solution)/shard_map/all_gather | solution.py:15
  367.8 4.0 fusion
  371.8 0.7 copy.5
  372.5 53.4 %all-gather.14.cloned.1.call-done = f32[128,2048]{0,1:T(8,128)} async-done(((f32[128,128]{0,1:T(8,128)}), f32[128,2048]{0,1:T(8,128)}) %all-gather.14.cloned.1.call-update) | async-done | bytes 1048592 | tf_op jit(solution)/shard_map/all_gather | solution.py:44
  426.0 3.7 fusion.4
  (14 shorter events, 0.2 us)
Async XLA Ops:
  7.2 0.7 copy-start.3
  7.2 93.7 %all-reduce.3.cloned.1.call-start = ((), (), s32[]{:S(2)}) async-start(), calls=%async_computation | async-start | bytes 524288 | tf_op jit(solution)/shard_map/psum | solution.py:27
  35.4 106.0 %all-reduce.5.cloned.1.call-start = ((), (), s32[]{:S(2)}) async-start(), calls=%async_computation.1 | async-start | bytes 524288 | tf_op jit(solution)/shard_map/psum | solution.py:27
  100.8 0.8 copy-start.2
  100.9 124.2 %all-gather.10.cloned.1.call-start = ((), (), s32[]{:S(2)}) async-start(), calls=%async_computation.4 | async-start | bytes 1179648 | tf_op jit(solution)/shard_map/all_gather | solution.py:15
  190.5 3.9 copy-start.1
  194.4 87.8 %all-gather.8.cloned.1.call-start = ((), (), s32[]{:S(2)}) async-start(), calls=%async_computation.3 | async-start | bytes 1114112 | tf_op jit(solution)/shard_map/all_gather | solution.py:44
  195.0 139.2 %all-gather.6.cloned.1.call-start = ((), (), s32[]{:S(2)}) async-start(), calls=%async_computation.2 | async-start | bytes 1114112 | tf_op jit(solution)/shard_map/all_gather | solution.py:44
  195.6 172.2 %all-gather.12.cloned.1.call-start = ((), (), s32[]{:S(2)}) async-start(), calls=%async_computation.5 | async-start | bytes 1179648 | tf_op jit(solution)/shard_map/all_gather | solution.py:15
  289.5 136.5 %copy-start = (f32[2048,128]{0,1:T(8,128)S(1)}, f32[2048,128]{0,1:T(8,128)}, u32[]{:S(2)}) copy-start(f32[2048,128]{0,1:T(8,128)} %all-gather.10.cloned.1.call-done) | copy-start | bytes 3145732
  289.5 136.5 %all-gather.14.cloned.1.call-start = ((), (), s32[]{:S(2)}) async-start(), calls=%async_computation.6 | async-start | bytes 1114112 | tf_op jit(solution)/shard_map/all_gather | solution.py:44
Sparse Core Ops, SparseCore 0:
  35.5 65.2 all-reduce.2
  103.4 37.9 all-reduce.4
  194.5 30.4 all-gather.9
  228.2 53.9 all-gather.7
  285.4 48.7 all-gather.5
  335.9 31.8 all-gather.11
  371.9 53.9 all-gather.13
where the time goes:
time: 437 us; the launch traced here: 436 us
  waiting for transfers between devices  324 us (74%)
  blocking collectives  80.1 us (18%)
  between operations  14.9 us (3%)
  matrix products  13.2 us (3%)
    all_gather x3, waiting for transfers between devices, panels(): whole_row = lax.all_gather(factor_one, GY, axis=1, tiled=True)  155 us
    psum x2, waiting for transfers between devices, spread(): array = lax.psum(array, axis)  105 us
    all_gather x2, waiting for transfers between devices, gather_axes(): filled = lax.all_gather(filled, axes[number], axis=dim, tiled=True)  63 us
    psum x5, blocking collectives, over_axes(): array = lax.psum(array, axis)  45.6 us
    all_gather x1, blocking collectives, local(): panel_rows = lax.all_gather(gradient, GY, axis=1, tiled=True)  26.8 us
    dot_general x4, matrix products, matmul(): jnp.dot(leading, trailing, preferred_element_type=jnp.float32, precision=...  13.2 us
  transfers between devices with their start and end apart: 7, of which 7 were waited for; matrix products, arithmetic and copies ran while one was open for 1% of the time, Pallas kernels for 0%

commit v1 on v0

v1 whole, which is shorter than its diff:
```python
import functools

import jax
import jax.numpy as jnp
from jax import lax
from jax.experimental import pallas as pl
from jax.experimental.pallas import tpu as pltpu
from jax.sharding import PartitionSpec as P

MESH = pl.DeviceIdType.MESH
N_GX = 16
N_GY = 16
B = 128
HALF = B // 2
PIECE = 32

COL_KEYS = (
    [("x", 0)]
    + [("z", d, st, h, s) for d in (0, 1) for st in (0, 1) for h in (0, 1) for s in (1, 2, 3, 4)
       if (h == 0 or st == 0) and (s < 4 or (d == 0) == (h == 0))]
    + [("xb", d, s) for d in (0, 1) for s in range(0, 5) if (d == 0 or s > 0) and (s < 4 or d == 1)]
)
ROW_KEYS = (
    [("x", 0)]
    + [("y", d, st, 1) for d in (0, 1) for st in (0, 1)]
    + [("y", d, st, 2) for d in (0, 1) for st in (0, 1)]
    + [("c", st, t) for st in (0, 1) for t in range(4)]
)
COL_AT = {key: number for number, key in enumerate(COL_KEYS)}
ROW_AT = {key: number for number, key in enumerate(ROW_KEYS)}


def split(x):
    high = x.astype(jnp.bfloat16)
    low = (x - high.astype(jnp.float32)).astype(jnp.bfloat16)
    return high, low


def dot3(a, b, dims=(((1,), (0,)), ((), ()))):
    a_high, a_low = split(a)
    b_high, b_low = split(b)
    dot = functools.partial(
        lax.dot_general, dimension_numbers=dims, preferred_element_type=jnp.float32
    )
    return dot(a_high, b_high) + (dot(a_high, b_low) + dot(a_low, b_high))


def wrap(value, count):
    return lax.rem(value + count, count)


def kernel(
    g_ref, o_ref, s_out, r_out,
    gi, gj, row1, col1, row2, col2, norms,
    gi_send, gi_recv, gj_send, gj_recv,
    c1_send, c1_recv, r1_send, r1_recv,
    c2_send, c2_recv, r2_send, r2_recv,
    n_send, n_recv, local_sem,
):
    i = lax.axis_index("gx")
    j = lax.axis_index("gy")
    ix = i + 1 - 2 * lax.rem(i, 2)
    jx = j + 2 - 4 * lax.rem(lax.div(j, 2), 2)
    jc = j + 1 - 2 * lax.rem(j, 2)
    pending = []

    def send(src, dst, send_sem, recv_sem, to):
        copy = pltpu.make_async_remote_copy(
            src_ref=src, dst_ref=dst, send_sem=send_sem, recv_sem=recv_sem,
            device_id=to, device_id_type=MESH,
        )
        copy.start()
        pending.append(copy)

    def arrived(dst, recv_sem, send_sem):
        pltpu.make_async_remote_copy(
            src_ref=dst, dst_ref=dst, send_sem=send_sem, recv_sem=recv_sem,
            device_id=(i, jc), device_id_type=MESH,
        ).wait_recv()

    barrier = pltpu.get_barrier_semaphore()

    def greet(to):
        pl.semaphore_signal(barrier, inc=1, device_id=to, device_id_type=MESH)

    for r in range(1, N_GY):
        greet((i, wrap(j + r, N_GY)))
    for r in range(1, N_GX):
        greet((wrap(i + r, N_GX), j))
    for r in range(1, N_GY):
        greet((j, wrap(j + r, N_GY)))

    @pl.when(i != j)
    def _():
        greet((j, j))

    mine = pl.ds(pl.multiple_of(j * PIECE, PIECE), PIECE)
    gi[mine, :] = g_ref[...].T

    @pl.when(i != j)
    def _():
        pl.semaphore_wait(barrier, 46)

    @pl.when(i == j)
    def _():
        pl.semaphore_wait(barrier, 45)

    first = pltpu.make_async_remote_copy(
        src_ref=gi.at[mine], dst_ref=gj.at[mine], send_sem=gj_send.at[0], recv_sem=gj_recv.at[j],
        device_id=(i, i), device_id_type=MESH,
    )
    here = pltpu.make_async_copy(gi.at[mine], gj.at[mine], local_sem)

    @pl.when(i != j)
    def _():
        first.start()

    @pl.when(i == j)
    def _():
        here.start()

    for r in range(1, N_GX):
        send(gi.at[mine], gj.at[mine], gj_send.at[r], gj_recv.at[j], (wrap(i + r, N_GX), i))
        send(gi.at[mine], gi.at[mine], gi_send.at[r], gi_recv.at[r], (i, wrap(j + r, N_GY)))
    for r in range(1, N_GY):
        m = wrap(j + N_GY - r, N_GY)
        part = pl.ds(pl.multiple_of(m * PIECE, PIECE), PIECE)
        arrived(gi.at[part], gi_recv.at[r], gi_send.at[r])
    for r in range(1, N_GY):
        m = wrap(j + r, N_GY)
        part = pl.ds(pl.multiple_of(m * PIECE, PIECE), PIECE)
        arrived(gj.at[part], gj_recv.at[m], gj_send.at[0])

    @pl.when(i != j)
    def _():
        arrived(gj.at[mine], gj_recv.at[j], gj_send.at[0])

    @pl.when(i == j)
    def _():
        here.wait()

    outer = dot3(gi[...], gj[...], (((0,), (0,)), ((), ())))
    stat = 0.9 * o_ref[...] + outer * (1.0 / (N_GY * PIECE))

    def gather(row, col, c_send, c_recv, r_send, r_recv):
        def col_part(slot, h):
            return col.at[slot, pl.ds(h * HALF, HALF)]

        def col_send(key, slot, h, to):
            q = COL_AT[key]
            send(col_part(slot, h), col_part(slot, h), c_send.at[q], c_recv.at[q], to)

        def col_wait(key, slot, h):
            q = COL_AT[key]
            arrived(col_part(slot, h), c_recv.at[q], c_send.at[q])

        def row_part(slot, h):
            return row.at[slot] if h is None else row.at[slot, pl.ds(h * HALF, HALF)]

        def row_send(key, slot, h, to):
            q = ROW_AT[key]
            send(row_part(slot, h), row_part(slot, h), r_send.at[q], r_recv.at[q], to)

        def row_wait(key, slot, h):
            q = ROW_AT[key]
            arrived(row_part(slot, h), r_recv.at[q], r_send.at[q])

        z_to = [(wrap(i + 2, 16), j), (wrap(i + 14, 16), j)]
        x_to = (ix, j)
        y_to = [(i, wrap(j + 4, 16)), (i, wrap(j + 12, 16))]
        h_to = (i, jx)
        c_to = (i, jc)
        z_off = [14, 2]
        y_off = [12, 4]

        def z_slot(base, d, s):
            return wrap(base + z_off[d] * s, 16)

        def y_slot(base, d, s):
            return wrap(base + y_off[d] * s, 16)

        col_send(("x", 0), i, 0, x_to)
        for d in (0, 1):
            col_send(("z", d, 0, 0, 1), i, 0, z_to[d])
        row_send(("x", 0), j, None, h_to)
        for d in (0, 1):
            row_send(("y", d, 0, 1), j, None, y_to[d])
        for d in (0, 1):
            col_send(("z", d, 0, 1, 1), i, 1, z_to[d])
        col_send(("xb", 0, 0), i, 1, x_to)
        row_send(("c", 0, 0), j, None, c_to)
        col_wait(("x", 0), ix, 0)
        for d in (0, 1):
            col_send(("z", d, 1, 0, 1), ix, 0, z_to[d])
        row_wait(("x", 0), jx, None)
        for d in (0, 1):
            row_send(("y", d, 1, 1), jx, None, y_to[d])
        row_send(("c", 1, 0), jx, None, c_to)
        for s in (1, 2, 3, 4):
            for h in (0, 1):
                for d in (0, 1):
                    if ("z", d, 0, h, s) not in COL_AT:
                        continue
                    slot = z_slot(i, d, s)
                    col_wait(("z", d, 0, h, s), slot, h)
                    if ("z", d, 0, h, s + 1) in COL_AT:
                        col_send(("z", d, 0, h, s + 1), slot, h, z_to[d])
                    if h == 1:
                        col_send(("xb", d, s), slot, h, x_to)
            for d in (0, 1):
                if ("z", d, 1, 0, s) not in COL_AT:
                    continue
                slot = z_slot(ix, d, s)
                col_wait(("z", d, 1, 0, s), slot, 0)
                if ("z", d, 1, 0, s + 1) in COL_AT:
                    col_send(("z", d, 1, 0, s + 1), slot, 0, z_to[d])
            for st, base in ((0, j), (1, jx)):
                if s == 1:
                    for d in (0, 1):
                        slot = y_slot(base, d, 1)
                        row_wait(("y", d, st, 1), slot, None)
                        row_send(("y", d, st, 2), slot, d, y_to[d])
                        row_send(("c", st, 1 + d), slot, None, c_to)
                if s == 2:
                    slot = y_slot(base, 0, 2)
                    for d in (0, 1):
                        row_wait(("y", d, st, 2), slot, d)
                    row_send(("c", st, 3), slot, None, c_to)
        for st, base in ((0, jc), (1, jx + jc - j)):
            for t, (d, s) in enumerate(((0, 0), (0, 1), (1, 1), (0, 2))):
                row_wait(("c", st, t), y_slot(base, d, s), None)
        for key in COL_KEYS:
            if key[0] == "xb":
                col_wait(key, z_slot(ix, key[1], key[2]), 1)

    row1[j] = stat
    col1[i] = stat
    s_out[...] = stat
    gather(row1, col1, c1_send, c1_recv, r1_send, r1_recv)

    squares = jnp.zeros((B, B), jnp.float32)
    for k in range(N_GY):
        squares = squares + row1[k] * row1[k]
    norms[i] = jnp.sum(squares, axis=0, keepdims=True)
    for r in range(1, N_GX):
        send(norms.at[i], norms.at[i], n_send.at[r], n_recv.at[r], (wrap(i + r, N_GX), j))

    def pair(ref, k, axis):
        return jnp.concatenate([ref[2 * k], ref[2 * k + 1]], axis=axis)

    power = jnp.zeros((B, B), jnp.float32)
    for k in range(N_GX // 2):
        power = power + dot3(pair(row1, k, 1), pair(col1, k, 0))
    row2[j] = power
    col2[i] = power
    gather(row2, col2, c2_send, c2_recv, r2_send, r2_recv)
    for r in range(1, N_GX):
        m = wrap(i + N_GX - r, N_GX)
        arrived(norms.at[m], n_recv.at[r], n_send.at[r])
    total = jnp.sum(jnp.sum(norms[...], axis=0), axis=1, keepdims=True)
    inv = 1.0 / (2.0 * jnp.sqrt(total * (1.0 / (N_GX * B))))
    inv2 = inv * inv
    c3 = -0.5625 * inv2 * inv
    c4 = 0.0625 * inv2 * inv2
    result = jnp.zeros((B, B), jnp.float32)
    for k in range(N_GX // 2):
        result = result + dot3(pair(row2, k, 1), c3 * pair(col1, k, 0) + c4 * pair(col2, k, 0))
    rows = lax.broadcasted_iota(jnp.int32, (B, B), 0)
    cols = lax.broadcasted_iota(jnp.int32, (B, B), 1)
    constant = jnp.where((rows == cols) & (i == j), 2.25, 0.0)
    r_out[...] = constant + (-2.4375 * inv) * s_out[...] + (1.6875 * inv2) * row2[j] + result

    @pl.when(i != j)
    def _():
        first.wait_send()

    for copy in pending:
        copy.wait_send()


def local(gradient, stat_old):
    dma = pltpu.SemaphoreType.DMA
    n_col, n_row = len(COL_KEYS), len(ROW_KEYS)
    block = jax.ShapeDtypeStruct((B, B), jnp.float32)
    return pl.pallas_call(
        kernel,
        out_shape=(block, block),
        in_specs=[pl.BlockSpec(memory_space=pltpu.VMEM)] * 2,
        out_specs=[pl.BlockSpec(memory_space=pltpu.VMEM)] * 2,
        scratch_shapes=[
            pltpu.VMEM((N_GY * PIECE, B), jnp.float32),
            pltpu.VMEM((N_GY * PIECE, B), jnp.float32),
            pltpu.VMEM((N_GY, B, B), jnp.float32),
            pltpu.VMEM((N_GX, B, B), jnp.float32),
            pltpu.VMEM((N_GY, B, B), jnp.float32),
            pltpu.VMEM((N_GX, B, B), jnp.float32),
            pltpu.VMEM((N_GX, 1, B), jnp.float32),
            dma((N_GX,)), dma((N_GX,)), dma((N_GX,)), dma((N_GX,)),
            dma((n_col,)), dma((n_col,)), dma((n_row,)), dma((n_row,)),
            dma((n_col,)), dma((n_col,)), dma((n_row,)), dma((n_row,)),
            dma((N_GX,)), dma((N_GX,)), dma(()),
        ],
        compiler_params=pltpu.CompilerParams(collective_id=0, has_side_effects=True),
        name="shampoo",
    )(gradient, stat_old)


def solution(mesh):
    placed = (P("gx", "gy"), P("gx", "gy"))
    return jax.shard_map(local, mesh=mesh, in_specs=placed, out_specs=placed, check_vma=False)
```

time: 437 us -> 68.6 us (0.16)
  the two profiles are of different devices: /device:TPU:1 before, /device:TPU:12 now
where the time goes in v1:
time: 68.6 us; the launch traced here: 68.4 us
  Pallas kernels  64.2 us (94%)
  local copies, waits for them, and re-layouts  3.59 us (5%)
    pallas_call x1, Pallas kernels, local(): pl.pallas_call(kernel, out_shape=(block, block), in_specs=[pl.BlockSpec(m...  64.2 us
    unnamed x5, local copies, waits for them, and re-layouts  3.59 us

profile of v1, /device:TPU:12, one launch (start us, length us, event | category | flops | bytes accessed | tf_op | source)
XLA Modules:
  0.0 68.4 jit_solution(11052903593829436358)
XLA Ops:
  0.6 1.4 %copy.4.g_ref = f32[128,32]{1,0:T(8,128)} copy(f32[128,32]{0,1:T(8,128)} %param.2) | data formatting | bytes 32768 | tf_op args[0]
  2.1 64.2 %shampoo.1 = (f32[128,128]{1,0:T(8,128)}, f32[128,128]{1,0:T(8,128)}) custom-call(f32[128,32]{1,0:T(8,128)} %copy.4.g_ref, f32[128,128]{1,0:T(8,128)} %o_ref.1), custom_call_target="tpu_custom_call" | custom-call | tf_op jit(solution)/shard_map/shampoo/pallas_call | solution.py:285
  66.2 0.0 copy-start
  66.2 1.5 %copy.7 = f32[128,128]{1,0:T(8,128)} copy(f32[128,128]{1,0:T(8,128)} %get-tuple-element.4) | data formatting | bytes 131072
  67.8 0.0 copy-done
  67.8 0.6 copy.8
Async XLA Ops:
  66.2 1.5 %copy-start = (f32[128,128]{1,0:T(8,128)S(1)}, f32[128,128]{1,0:T(8,128)}, u32[]{:S(2)}) copy-start(f32[128,128]{1,0:T(8,128)} %get-tuple-element.5) | copy-start | bytes 196612

commit v2 on v0

v2 whole, which is shorter than its diff:
```python
import functools

import jax
import jax.numpy as jnp
from jax import lax
from jax.experimental import pallas as pl
from jax.experimental.pallas import tpu as pltpu
from jax.sharding import PartitionSpec as P

MESH = pl.DeviceIdType.MESH
N = 16
B = 128
HALF = B // 2
PIECE = 32
STEPS = (1, 3, 2)

ROW_KEYS = (
    [("x", dx, h) for dx in STEPS for h in (0, 1)]
    + [("y", dy, h) for dy in STEPS for h in (0, 1)]
    + [("xy", dx, dy) for dx in STEPS for dy in STEPS]
    + [("yx", dx, dy) for dx in STEPS for dy in STEPS]
)
COL_KEYS = (
    [("z", 2, d, h) for d in (0, 1) for h in (0, 1)]
    + [("z", 1, d) for d in (0, 1)]
    + [("z", 3, d, h) for d in (0, 1) for h in (0, 1)]
    + [("z", 4, d) for d in (0, 1)]
    + [("c", dz) for dz in range(8)]
)
ROW_AT = {key: number for number, key in enumerate(ROW_KEYS)}
COL_AT = {key: number for number, key in enumerate(COL_KEYS)}


def split(x):
    high = x.astype(jnp.bfloat16)
    low = (x - high.astype(jnp.float32)).astype(jnp.bfloat16)
    return high, low


def dot3(a, b, dims=(((1,), (0,)), ((), ()))):
    a_high, a_low = split(a)
    b_high, b_low = split(b)
    dot = functools.partial(
        lax.dot_general, dimension_numbers=dims, preferred_element_type=jnp.float32
    )
    return dot(a_high, b_high) + (dot(a_high, b_low) + dot(a_low, b_high))


def kernel(
    g_hbm, o_hbm, s_out, r_out,
    g_own, o_own, o_far, s_far, r_own, r_far,
    gi, gj, row1, col1, row2, col2, norms,
    local_sem, g_send, gi_recv, gj_recv, gc_recv,
    c_send, r_send, c1_recv, r1_recv, c2_recv, r2_recv,
    n_send, n_recv, swap_send, swap_recv,
):
    i = lax.axis_index("gx")
    j = lax.axis_index("gy")
    z, xl = lax.div(i, 2), lax.rem(i, 2)
    y, xh, c = lax.div(j, 4), lax.rem(lax.div(j, 2), 2), lax.rem(j, 2)
    x = xh * 2 + xl
    ti = z * 2 + c
    tj = y * 4 + x
    swapped = c != xl

    def at(pz, px, py, pc):
        return (pz * 2 + lax.rem(px, 2), py * 4 + lax.div(px, 2) * 2 + pc)

    def step(value, by, size):
        return lax.rem(value + by, size)

    def remote(src, dst, send_sem, recv_sem, to):
        return pltpu.make_async_remote_copy(
            src_ref=src, dst_ref=dst, send_sem=send_sem, recv_sem=recv_sem,
            device_id=to, device_id_type=MESH,
        )

    def bytes_of(ref, sem):
        pltpu.make_async_copy(ref, ref, sem).wait()

    g_in = pltpu.make_async_copy(g_hbm, g_own, local_sem.at[0])
    o_in = pltpu.make_async_copy(o_hbm, o_own, local_sem.at[1])
    g_in.start()
    o_in.start()

    barrier = pltpu.get_barrier_semaphore()

    def greet(to):
        pl.semaphore_signal(barrier, inc=1, device_id=to, device_id_type=MESH)

    for r in range(1, N):
        greet((ti, step(j, r, N)))

    @pl.when(swapped)
    def _():
        greet((ti, j))
        greet((ti, tj))

    for r in range(1, 8):
        greet((tj, step(j, 2 * r, N)))

    @pl.when(i != tj)
    def _():
        greet((tj, j))

    for s in STEPS:
        greet(at(z, step(x, s, 4), y, c))
        greet(at(z, x, step(y, s, 4), c))
    for s in range(1, 8):
        greet(at(step(z, s, 8), x, y, c))
    for s in range(8):
        greet(at(step(z, s, 8), x, y, 1 - c))
    g_in.wait()
    same = 1 - (c - xl) * (c - xl)
    pl.semaphore_wait(barrier, 46 - 2 * same - (i == tj).astype(jnp.int32))

    order = lax.rem(j, 2) * 8 + lax.div(j, 2)
    mine = pl.ds(pl.multiple_of(order * PIECE, PIECE), PIECE)
    ky, kx = lax.div(i, 4), lax.rem(i, 4)
    gi_near = remote(g_own, gi.at[mine], g_send, gi_recv, (i, y * 4 + xh * 2 + xl))
    gj_near = remote(g_own, gj.at[mine], g_send, gj_recv, at(z, kx, ky, c))
    gi_here = pltpu.make_async_copy(g_own, gi.at[mine], local_sem.at[0])
    gj_here = pltpu.make_async_copy(g_own, gj.at[mine], local_sem.at[2])

    for r in range(1, 8):
        remote(g_own, gj.at[mine], g_send, gj_recv, at(step(z, r, 8), kx, ky, c)).start()

    @pl.when(i != tj)
    def _():
        gj_near.start()

    @pl.when(i == tj)
    def _():
        gj_here.start()

    for r in range(N):
        sx, sy = r % 4, r // 4
        if r:
            remote(
                g_own, gi.at[mine], g_send, gi_recv, at(z, step(x, sx, 4), step(y, sy, 4), xl)
            ).start()

    @pl.when(swapped)
    def _():
        gi_near.start()

    @pl.when(jnp.logical_not(swapped))
    def _():
        gi_here.start()

    o_in.wait()
    o_swap = remote(o_own, o_far, swap_send.at[0], swap_recv.at[0], (ti, tj))

    @pl.when(swapped)
    def _():
        o_swap.start()

    quarter = 8 * PIECE

    @pl.when(i != tj)
    def _():
        bytes_of(gj.at[pl.ds(0, quarter)], gj_recv)

    @pl.when(i == tj)
    def _():
        bytes_of(gj.at[pl.ds(0, quarter - PIECE)], gj_recv)
        gj_here.wait()

    mine_half = pl.ds(pl.multiple_of(c * quarter, quarter), quarter)
    other_half = pl.ds(pl.multiple_of((1 - c) * quarter, quarter), quarter)
    gj_share = remote(gj.at[mine_half], gj.at[mine_half], g_send, gc_recv, (i, j + 1 - 2 * c))
    gj_share.start()

    @pl.when(swapped)
    def _():
        bytes_of(gi, gi_recv)

    @pl.when(jnp.logical_not(swapped))
    def _():
        bytes_of(gi.at[pl.ds(0, 15 * PIECE)], gi_recv)
        gi_here.wait()

    remote(
        gj.at[other_half], gj.at[other_half], g_send, gc_recv, (i, j + 1 - 2 * c)
    ).wait_recv()

    outer = dot3(gi[...], gj[...], (((0,), (0,)), ((), ())))

    @pl.when(swapped)
    def _():
        o_swap.wait_send()
        o_swap.wait_recv()
        o_own[...] = o_far[...]

    stat = 0.9 * o_own[...] + outer * (1.0 / (N * PIECE))

    def gather(row, col, c_send, c_recv, r_send, r_recv):
        def row_part(slot, h):
            return row.at[slot, pl.ds(h * HALF, HALF)]

        def row_send(key, slot, h, to):
            part = row_part(slot, h)
            remote(part, part, r_send, r_recv.at[ROW_AT[key]], to).start()

        def row_wait(key, slot, h):
            part = row_part(slot, h)
            remote(part, part, r_send, r_recv.at[ROW_AT[key]], (i, j + 1 - 2 * c)).wait_recv()

        def col_part(slot, h):
            return col.at[slot] if h is None else col.at[slot, pl.ds(h * HALF, HALF)]

        def col_send(key, slot, h, to):
            part = col_part(slot, h)
            remote(part, part, c_send, c_recv.at[COL_AT[key]], to).start()

        def col_wait(key, slot, h):
            part = col_part(slot, h)
            remote(part, part, c_send, c_recv.at[COL_AT[key]], (i, j + 1 - 2 * c)).wait_recv()

        def x_to(s):
            return at(z, step(x, s, 4), y, c)

        def y_to(s):
            return at(z, x, step(y, s, 4), c)

        def z_to(s):
            return at(step(z, s, 8), x, y, c)

        def from_xy(dx, dy):
            return step(y, 4 - dy, 4) * 4 + step(x, 4 - dx, 4)

        def from_z(dz, core):
            return step(z, 8 - dz, 8) * 2 + core

        other = (i, j + 1 - 2 * c)
        away = (2, 6)
        near = (1, 7)
        for h in (0, 1):
            for d in (0, 1):
                col_send(("z", 2, d, h), ti, h, z_to(away[d]))
            for s in STEPS:
                row_send(("x", s, h), tj, h, x_to(s))
                row_send(("y", s, 1 - h), tj, 1 - h, y_to(s))
        for d in (0, 1):
            col_send(("z", 1, d), ti, None, z_to(near[d]))
        col_send(("c", 0), ti, None, other)

        for s in STEPS:
            row_wait(("x", s, 0), from_xy(s, 0), 0)
            for t in STEPS:
                row_send(("xy", s, t), from_xy(s, 0), 0, y_to(t))
            row_wait(("y", s, 1), from_xy(0, s), 1)
            for t in STEPS:
                row_send(("yx", t, s), from_xy(0, s), 1, x_to(t))
        for h in (0, 1):
            for d in (0, 1):
                slot = from_z(away[d], c)
                col_wait(("z", 2, d, h), slot, h)
                if h == d:
                    col_send(("z", 4, d), slot, h, z_to(away[d]))
                col_send(("z", 3, d, h), slot, h, z_to(near[d]))
        for d in (0, 1):
            col_send(("c", away[d]), from_z(away[d], c), None, other)
        for d in (0, 1):
            col_wait(("z", 1, d), from_z(near[d], c), None)
            col_send(("c", near[d]), from_z(near[d], c), None, other)
        for d in (0, 1):
            slot = from_z((away[d] + near[d]) % 8, c)
            for h in (0, 1):
                col_wait(("z", 3, d, h), slot, h)
            col_send(("c", (away[d] + near[d]) % 8), slot, None, other)
        for d in (0, 1):
            col_wait(("z", 4, d), from_z(4, c), d)
        col_send(("c", 4), from_z(4, c), None, other)
        for s in STEPS:
            row_wait(("x", s, 1), from_xy(s, 0), 1)
            row_wait(("y", s, 0), from_xy(0, s), 0)
        for s in STEPS:
            for t in STEPS:
                row_wait(("xy", s, t), from_xy(s, t), 0)
                row_wait(("yx", t, s), from_xy(t, s), 1)
        for dz in range(8):
            col_wait(("c", dz), from_z(dz, 1 - c), None)

    row1[tj] = stat
    col1[ti] = stat
    s_out[...] = stat
    gather(row1, col1, c_send.at[0], c1_recv, r_send.at[0], r1_recv)
    s_swap = remote(row1.at[tj], s_far, swap_send.at[1], swap_recv.at[1], (ti, tj))

    @pl.when(swapped)
    def _():
        s_swap.start()

    squares = jnp.zeros((B, B), jnp.float32)
    for k in range(N):
        squares = squares + row1[k] * row1[k]
    norms[ti] = jnp.sum(squares, axis=0, keepdims=True)
    for r in range(1, N):
        remote(
            norms.at[ti], norms.at[ti], n_send, n_recv,
            at(step(z, r // 2, 8), x, y, step(c, r % 2, 2)),
        ).start()

    def pair(ref, k, axis):
        return jnp.concatenate([ref[2 * k], ref[2 * k + 1]], axis=axis)

    power = jnp.zeros((B, B), jnp.float32)
    for k in range(N // 2):
        power = power + dot3(pair(row1, k, 1), pair(col1, k, 0))
    row2[tj] = power
    col2[ti] = power
    gather(row2, col2, c_send.at[1], c2_recv, r_send.at[1], r2_recv)
    bytes_of(norms.at[pl.ds(0, N - 1)], n_recv)
    total = jnp.sum(jnp.sum(norms[...], axis=0), axis=1, keepdims=True)
    inv = 1.0 / (2.0 * jnp.sqrt(total * (1.0 / (N * B))))
    inv2 = inv * inv
    c3 = -0.5625 * inv2 * inv
    c4 = 0.0625 * inv2 * inv2
    result = jnp.zeros((B, B), jnp.float32)
    for k in range(N // 2):
        result = result + dot3(pair(row2, k, 1), c3 * pair(col1, k, 0) + c4 * pair(col2, k, 0))
    rows = lax.broadcasted_iota(jnp.int32, (B, B), 0)
    cols = lax.broadcasted_iota(jnp.int32, (B, B), 1)
    constant = jnp.where((rows == cols) & (ti == tj), 2.25, 0.0)
    result = constant + (-2.4375 * inv) * row1[tj] + (1.6875 * inv2) * row2[tj] + result
    r_own[...] = result
    r_out[...] = result
    r_swap = remote(r_own, r_far, swap_send.at[2], swap_recv.at[2], (ti, tj))

    @pl.when(swapped)
    def _():
        r_swap.start()
        s_swap.wait_send()
        s_swap.wait_recv()
        s_out[...] = s_far[...]

    for phase, (row, col) in enumerate(((row1, col1), (row2, col2))):
        bytes_of(row.at[pl.ds(0, 15)], r_send.at[phase])
        bytes_of(col.at[pl.ds(0, 15)], c_send.at[phase])
    bytes_of(norms.at[pl.ds(0, N - 1)], n_send)
    bytes_of(gj.at[pl.ds(0, quarter)], g_send)
    bytes_of(gi.at[pl.ds(0, 22 * PIECE - 8 * PIECE)], g_send)
    bytes_of(gj.at[pl.ds(0, 8 * PIECE)], g_send)

    @pl.when(swapped)
    def _():
        bytes_of(g_own, g_send)

    @pl.when(i != tj)
    def _():
        bytes_of(g_own, g_send)

    @pl.when(swapped)
    def _():
        r_swap.wait_send()
        r_swap.wait_recv()
        r_out[...] = r_far[...]


def local(gradient, stat_old):
    dma = pltpu.SemaphoreType.DMA
    n_col, n_row = len(COL_KEYS), len(ROW_KEYS)
    block = jax.ShapeDtypeStruct((B, B), jnp.float32)
    tile = pltpu.VMEM((B, B), jnp.float32)
    panel = pltpu.VMEM((N, B, B), jnp.float32)
    pieces = pltpu.VMEM((N * PIECE, B), jnp.float32)
    return pl.pallas_call(
        kernel,
        out_shape=(block, block),
        in_specs=[pl.BlockSpec(memory_space=pltpu.HBM)] * 2,
        out_specs=[pl.BlockSpec(memory_space=pltpu.VMEM)] * 2,
        scratch_shapes=[
            pltpu.VMEM((PIECE, B), jnp.float32), tile, tile, tile, tile, tile,
            pieces, pieces, panel, panel, panel, panel, pltpu.VMEM((N, 1, B), jnp.float32),
            dma((3,)), dma(()), dma(()), dma(()), dma(()),
            dma((2,)), dma((2,)), dma((n_col,)), dma((n_row,)), dma((n_col,)), dma((n_row,)),
            dma(()), dma(()), dma((3,)), dma((3,)),
        ],
        compiler_params=pltpu.CompilerParams(
            collective_id=0, has_side_effects=True, vmem_limit_bytes=16 * 1024 * 1024
        ),
        name="shampoo",
    )(gradient.T, stat_old)


def solution(mesh):
    placed = (P("gx", "gy"), P("gx", "gy"))
    return jax.shard_map(local, mesh=mesh, in_specs=placed, out_specs=placed, check_vma=False)
```

time: 437 us -> 50.8 us (0.12)
  waiting for transfers between devices: 324 us -> 0 us
  blocking collectives: 80.1 us -> 0 us
  Pallas kernels: 0 us -> 47.2 us
  between operations: 14.9 us -> 0.65 us
  matrix products: 13.2 us -> 0 us
    all_gather x5 -> x0, waiting for transfers between devices: 218 us -> none  [the longest x3 155 us: panels(): whole_row = lax.all_gather(factor_one, GY, axis=1, tiled=True)]
    psum x2 -> x0, waiting for transfers between devices: 105 us -> none  [spread(): array = lax.psum(array, axis)]
    pallas_call x0 -> x1, Pallas kernels: none -> 47.2 us  [local(): pl.pallas_call(kernel, out_shape=(block, block), in_specs=[pl.BlockSpec(m...]
    psum x5 -> x0, blocking collectives: 45.6 us -> none  [over_axes(): array = lax.psum(array, axis)]
    all_gather x3 -> x0, blocking collectives: 34.5 us -> none  [the longest x1 26.8 us: local(): panel_rows = lax.all_gather(gradient, GY, axis=1, tiled=True)]
    dot_general x4 -> x0, matrix products: 13.2 us -> none  [matmul(): jnp.dot(leading, trailing, preferred_element_type=jnp.float32, precision=...]
  transfers between devices with their start and end apart: 7 -> 0, of which waited for: 7 -> 0; matrix products, arithmetic and copies ran while one was open for 1% -> 0% of each run, Pallas kernels for 0% -> 0%
where the time goes in v2:
time: 50.8 us; the launch traced here: 50.6 us
  Pallas kernels  47.2 us (93%)
  local copies, waits for them, and re-layouts  2.81 us (6%)
  between operations  0.65 us (1%)
    pallas_call x1, Pallas kernels, local(): pl.pallas_call(kernel, out_shape=(block, block), in_specs=[pl.BlockSpec(m...  47.2 us
    unnamed x6, local copies, waits for them, and re-layouts  2.81 us

profile of v2, /device:TPU:1, one launch (start us, length us, event | category | flops | bytes accessed | tf_op | source)
XLA Modules:
  0.0 50.6 jit_solution(7175173043222874185)
XLA Ops:
  0.6 0.0 copy-start
  0.6 0.8 %copy-done = f32[128,128]{1,0:T(8,128)S(1)} copy-done((f32[128,128]{1,0:T(8,128)S(1)}, f32[128,128]{1,0:T(8,128)}, u32[]{:S(2)}) %copy-start) | copy-done | bytes 65560
  1.5 0.0 copy-start.1
  1.5 0.7 %copy-done.1 = f32[128,32]{0,1:T(8,128)S(1)} copy-done((f32[128,32]{0,1:T(8,128)S(1)}, f32[128,32]{0,1:T(8,128)}, u32[]{:S(2)}) %copy-start.1) | copy-done | bytes 16408
  2.2 47.2 %shampoo.1 = (f32[128,128]{1,0:T(8,128)S(1)}, f32[128,128]{1,0:T(8,128)S(1)}) custom-call(f32[32,128]{1,0:T(8,128)S(1)} %bitcast.1, f32[128,128]{1,0:T(8,128)S(1)} %copy-done), custom_call_target="tpu_custom_call" | custom-call | tf_op jit(solution)/shard_map/shampoo/pallas_call | solution.py:368
  49.4 0.6 %copy.6 = f32[128,128]{1,0:T(8,128)} copy(f32[128,128]{1,0:T(8,128)S(1)} %get-tuple-element.4) | data formatting | bytes 131072
  50.0 0.6 %copy.7 = f32[128,128]{1,0:T(8,128)} copy(f32[128,128]{1,0:T(8,128)S(1)} %get-tuple-element.5) | data formatting | bytes 131072
Async XLA Ops:
  0.6 0.8 %copy-start = (f32[128,128]{1,0:T(8,128)S(1)}, f32[128,128]{1,0:T(8,128)}, u32[]{:S(2)}) copy-start(f32[128,128]{1,0:T(8,128)} %o_hbm.1) | copy-start | bytes 196612
  1.5 0.7 %copy-start.1 = (f32[128,32]{0,1:T(8,128)S(1)}, f32[128,32]{0,1:T(8,128)}, u32[]{:S(2)}) copy-start(f32[128,32]{0,1:T(8,128)} %param.2) | copy-start | bytes 49156

commit v3 on v2

--- a/solution.py
+++ b/solution.py
@@ -14,18 +14,10 @@
 PIECE = 32
 STEPS = (1, 3, 2)
 
-ROW_KEYS = (
-    [("x", dx, h) for dx in STEPS for h in (0, 1)]
-    + [("y", dy, h) for dy in STEPS for h in (0, 1)]
-    + [("xy", dx, dy) for dx in STEPS for dy in STEPS]
-    + [("yx", dx, dy) for dx in STEPS for dy in STEPS]
-)
+ROW_KEYS = [("x", s) for s in STEPS] + [("y", s) for s in STEPS] + ["rest"]
 COL_KEYS = (
     [("z", 2, d, h) for d in (0, 1) for h in (0, 1)]
-    + [("z", 1, d) for d in (0, 1)]
-    + [("z", 3, d, h) for d in (0, 1) for h in (0, 1)]
-    + [("z", 4, d) for d in (0, 1)]
-    + [("c", dz) for dz in range(8)]
+    + [("z", 1), ("z", 3, 0), ("z", 3, 1), ("z", 4), "near", "far"]
 )
 ROW_AT = {key: number for number, key in enumerate(ROW_KEYS)}
 COL_AT = {key: number for number, key in enumerate(COL_KEYS)}
@@ -88,6 +80,13 @@
     def greet(to):
         pl.semaphore_signal(barrier, inc=1, device_id=to, device_id_type=MESH)
 
+    for r in range(1, 8):
+        greet((tj, step(j, 2 * r, N)))
+
+    @pl.when(i != tj)
+    def _():
+        greet((tj, j))
+
     for r in range(1, N):
         greet((ti, step(j, r, N)))
 
@@ -95,13 +94,6 @@
     def _():
         greet((ti, j))
         greet((ti, tj))
-
-    for r in range(1, 8):
-        greet((tj, step(j, 2 * r, N)))
-
-    @pl.when(i != tj)
-    def _():
-        greet((tj, j))
 
     for s in STEPS:
         greet(at(z, step(x, s, 4), y, c))
@@ -194,17 +186,13 @@
 
     stat = 0.9 * o_own[...] + outer * (1.0 / (N * PIECE))
 
-    def gather(row, col, c_send, c_recv, r_send, r_recv):
-        def row_part(slot, h):
-            return row.at[slot, pl.ds(h * HALF, HALF)]
-
+    def gather(row, col, c_send, c_recv, r_send, r_recv, between, product):
         def row_send(key, slot, h, to):
-            part = row_part(slot, h)
+            part = row.at[slot, pl.ds(h * HALF, HALF)]
             remote(part, part, r_send, r_recv.at[ROW_AT[key]], to).start()
 
-        def row_wait(key, slot, h):
-            part = row_part(slot, h)
-            remote(part, part, r_send, r_recv.at[ROW_AT[key]], (i, j + 1 - 2 * c)).wait_recv()
+        def row_wait(key, tiles):
+            bytes_of(tiles, r_recv.at[ROW_AT[key]])
 
         def col_part(slot, h):
             return col.at[slot] if h is None else col.at[slot, pl.ds(h * HALF, HALF)]
@@ -213,9 +201,8 @@
             part = col_part(slot, h)
             remote(part, part, c_send, c_recv.at[COL_AT[key]], to).start()
 
-        def col_wait(key, slot, h):
-            part = col_part(slot, h)
-            remote(part, part, c_send, c_recv.at[COL_AT[key]], (i, j + 1 - 2 * c)).wait_recv()
+        def col_wait(key, tiles):
+            bytes_of(tiles, c_recv.at[COL_AT[key]])
 
         def x_to(s):
             return at(z, step(x, s, 4), y, c)
@@ -239,87 +226,98 @@
             for d in (0, 1):
                 col_send(("z", 2, d, h), ti, h, z_to(away[d]))
             for s in STEPS:
-                row_send(("x", s, h), tj, h, x_to(s))
-                row_send(("y", s, 1 - h), tj, 1 - h, y_to(s))
+                row_send(("x", s) if h == 0 else "rest", tj, h, x_to(s))
+                row_send(("y", s) if h == 0 else "rest", tj, 1 - h, y_to(s))
         for d in (0, 1):
-            col_send(("z", 1, d), ti, None, z_to(near[d]))
-        col_send(("c", 0), ti, None, other)
-
+            col_send(("z", 1), ti, None, z_to(near[d]))
+        col_send("near", ti, None, other)
+        between()
+
+        half = row.at[0, pl.ds(0, HALF)]
         for s in STEPS:
-            row_wait(("x", s, 0), from_xy(s, 0), 0)
+            row_wait(("x", s), half)
             for t in STEPS:
-                row_send(("xy", s, t), from_xy(s, 0), 0, y_to(t))
-            row_wait(("y", s, 1), from_xy(0, s), 1)
+                row_send("rest", from_xy(s, 0), 0, y_to(t))
+            row_wait(("y", s), half)
             for t in STEPS:
-                row_send(("yx", t, s), from_xy(0, s), 1, x_to(t))
+                row_send("rest", from_xy(0, s), 1, x_to(t))
         for h in (0, 1):
             for d in (0, 1):
                 slot = from_z(away[d], c)
-                col_wait(("z", 2, d, h), slot, h)
+                col_wait(("z", 2, d, h), half)
                 if h == d:
-                    col_send(("z", 4, d), slot, h, z_to(away[d]))
-                col_send(("z", 3, d, h), slot, h, z_to(near[d]))
+                    col_send(("z", 4), slot, h, z_to(away[d]))
+                col_send(("z", 3, d), slot, h, z_to(near[d]))
         for d in (0, 1):
-            col_send(("c", away[d]), from_z(away[d], c), None, other)
+            col_send("near", from_z(away[d], c), None, other)
+        col_wait(("z", 1), col.at[pl.ds(0, 2)])
         for d in (0, 1):
-            col_wait(("z", 1, d), from_z(near[d], c), None)
-            col_send(("c", near[d]), from_z(near[d], c), None, other)
+            col_send("near", from_z(near[d], c), None, other)
         for d in (0, 1):
-            slot = from_z((away[d] + near[d]) % 8, c)
-            for h in (0, 1):
-                col_wait(("z", 3, d, h), slot, h)
-            col_send(("c", (away[d] + near[d]) % 8), slot, None, other)
-        for d in (0, 1):
-            col_wait(("z", 4, d), from_z(4, c), d)
-        col_send(("c", 4), from_z(4, c), None, other)
-        for s in STEPS:
-            row_wait(("x", s, 1), from_xy(s, 0), 1)
-            row_wait(("y", s, 0), from_xy(0, s), 0)
-        for s in STEPS:
-            for t in STEPS:
-                row_wait(("xy", s, t), from_xy(s, t), 0)
-                row_wait(("yx", t, s), from_xy(t, s), 1)
-        for dz in range(8):
-            col_wait(("c", dz), from_z(dz, 1 - c), None)
+            col_wait(("z", 3, d), col.at[0])
+            col_send("far", from_z((away[d] + near[d]) % 8, c), None, other)
+        col_wait(("z", 4), col.at[0])
+        col_send("far", from_z(4, c), None, other)
+        row_wait("rest", row.at[pl.ds(0, 12)])
+        col_wait("near", col.at[pl.ds(0, 5)])
+        total = product(step(z, 0, 8))
+        for dz in (1, 7, 2, 6):
+            total = total + product(step(z, dz, 8))
+        col_wait("far", col.at[pl.ds(0, 3)])
+        for dz in (3, 5, 4):
+            total = total + product(step(z, dz, 8))
+        return total
 
     row1[tj] = stat
     col1[ti] = stat
-    s_out[...] = stat
-    gather(row1, col1, c_send.at[0], c1_recv, r_send.at[0], r1_recv)
     s_swap = remote(row1.at[tj], s_far, swap_send.at[1], swap_recv.at[1], (ti, tj))
-
-    @pl.when(swapped)
-    def _():
-        s_swap.start()
-
-    squares = jnp.zeros((B, B), jnp.float32)
-    for k in range(N):
-        squares = squares + row1[k] * row1[k]
-    norms[ti] = jnp.sum(squares, axis=0, keepdims=True)
-    for r in range(1, N):
-        remote(
-            norms.at[ti], norms.at[ti], n_send, n_recv,
-            at(step(z, r // 2, 8), x, y, step(c, r % 2, 2)),
-        ).start()
 
     def pair(ref, k, axis):
         return jnp.concatenate([ref[2 * k], ref[2 * k + 1]], axis=axis)
 
-    power = jnp.zeros((B, B), jnp.float32)
-    for k in range(N // 2):
-        power = power + dot3(pair(row1, k, 1), pair(col1, k, 0))
+    def keep_stat():
+        s_out[...] = stat
+
+        @pl.when(swapped)
+        def _():
+            s_swap.start()
+
+    def square(k):
+        return dot3(pair(row1, k, 1), pair(col1, k, 0))
+
+    power = gather(
+        row1, col1, c_send.at[0], c1_recv, r_send.at[0], r1_recv, keep_stat, square
+    )
     row2[tj] = power
     col2[ti] = power
-    gather(row2, col2, c_send.at[1], c2_recv, r_send.at[1], r2_recv)
-    bytes_of(norms.at[pl.ds(0, N - 1)], n_recv)
-    total = jnp.sum(jnp.sum(norms[...], axis=0), axis=1, keepdims=True)
-    inv = 1.0 / (2.0 * jnp.sqrt(total * (1.0 / (N * B))))
-    inv2 = inv * inv
-    c3 = -0.5625 * inv2 * inv
-    c4 = 0.0625 * inv2 * inv2
-    result = jnp.zeros((B, B), jnp.float32)
-    for k in range(N // 2):
-        result = result + dot3(pair(row2, k, 1), c3 * pair(col1, k, 0) + c4 * pair(col2, k, 0))
+
+    def send_norms():
+        squares = jnp.zeros((B, B), jnp.float32)
+        for k in range(N):
+            squares = squares + row1[k] * row1[k]
+        norms[ti] = jnp.sum(squares, axis=0, keepdims=True)
+        for r in range(1, N):
+            remote(
+                norms.at[ti], norms.at[ti], n_send, n_recv,
+                at(step(z, r // 2, 8), x, y, step(c, r % 2, 2)),
+            ).start()
+
+    scales = []
+
+    def last(k):
+        if not scales:
+            bytes_of(norms.at[pl.ds(0, N - 1)], n_recv)
+            total = jnp.sum(jnp.sum(norms[...], axis=0), axis=1, keepdims=True)
+            inv = 1.0 / (2.0 * jnp.sqrt(total * (1.0 / (N * B))))
+            scales.extend((inv, inv * inv))
+        inv, inv2 = scales
+        factor = (-0.5625 * inv2 * inv) * pair(col1, k, 0) + (0.0625 * inv2 * inv2) * pair(col2, k, 0)
+        return dot3(pair(row2, k, 1), factor)
+
+    result = gather(
+        row2, col2, c_send.at[1], c2_recv, r_send.at[1], r2_recv, send_norms, last
+    )
+    inv, inv2 = scales
     rows = lax.broadcasted_iota(jnp.int32, (B, B), 0)
     cols = lax.broadcasted_iota(jnp.int32, (B, B), 1)
     constant = jnp.where((rows == cols) & (ti == tj), 2.25, 0.0)
@@ -358,6 +356,17 @@
         r_out[...] = r_far[...]
 
 
+def store(s_ref, r_ref, s_hbm, r_hbm, sems):
+    copies = [
+        pltpu.make_async_copy(s_ref, s_hbm, sems.at[0]),
+        pltpu.make_async_copy(r_ref, r_hbm, sems.at[1]),
+    ]
+    for copy in copies:
+        copy.start()
+    for copy in copies:
+        copy.wait()
+
+
 def local(gradient, stat_old):
     dma = pltpu.SemaphoreType.DMA
     n_col, n_row = len(COL_KEYS), len(ROW_KEYS)
@@ -365,7 +374,7 @@
     tile = pltpu.VMEM((B, B), jnp.float32)
     panel = pltpu.VMEM((N, B, B), jnp.float32)
     pieces = pltpu.VMEM((N * PIECE, B), jnp.float32)
-    return pl.pallas_call(
+    made = pl.pallas_call(
         kernel,
         out_shape=(block, block),
         in_specs=[pl.BlockSpec(memory_space=pltpu.HBM)] * 2,
@@ -381,7 +390,19 @@
             collective_id=0, has_side_effects=True, vmem_limit_bytes=16 * 1024 * 1024
         ),
         name="shampoo",
-    )(gradient.T, stat_old)
+    )(
+        pltpu.with_memory_space_constraint(gradient.T, pltpu.HBM),
+        pltpu.with_memory_space_constraint(stat_old, pltpu.HBM),
+    )
+    return pl.pallas_call(
+        store,
+        out_shape=(block, block),
+        in_specs=[pl.BlockSpec(memory_space=pltpu.VMEM)] * 2,
+        out_specs=[pl.BlockSpec(memory_space=pltpu.HBM)] * 2,
+        scratch_shapes=[dma((2,))],
+        compiler_params=pltpu.CompilerParams(vmem_limit_bytes=1024 * 1024),
+        name="store",
+    )(*made)
 
 
 def solution(mesh):

time: 50.8 us -> 48 us (0.945)
  local copies, waits for them, and re-layouts: 2.81 us -> 0 us
    unnamed x6 -> x0, local copies, waits for them, and re-layouts: 2.81 us -> none
    pallas_call x0 -> x1, Pallas kernels: none -> 0.67 us  [local(): pl.pallas_call(store, out_shape=(block, block), in_specs=[pl.BlockSpec(me...]
    pallas_call x1, Pallas kernels: 47.2 us -> 46.6 us  [local(): pl.pallas_call(kernel, out_shape=(block, block), in_specs=[pl.BlockSpec(m...]
where the time goes in v3:
time: 48 us; the launch traced here: 47.9 us
  Pallas kernels  47.2 us (98%)
  between operations  0.64 us (1%)
    pallas_call x1, Pallas kernels, local(): pl.pallas_call(kernel, out_shape=(block, block), in_specs=[pl.BlockSpec(m...  46.6 us

profile of v3, /device:TPU:1, one launch (start us, length us, event | category | flops | bytes accessed | tf_op | source)
XLA Modules:
  0.0 47.9 jit_solution(14991110674994013284)
XLA Ops:
  0.6 46.6 %shampoo.1 = (f32[128,128]{1,0:T(8,128)S(1)}, f32[128,128]{1,0:T(8,128)S(1)}) custom-call(f32[32,128]{1,0:T(8,128)} %bitcast.1, f32[128,128]{1,0:T(8,128)} %o_hbm.1), custom_call_target="tpu_custom_call" | custom-call | tf_op jit(solution)/shard_map/shampoo/pallas_call | solution.py:377
  47.2 0.7 %store.1 = (f32[128,128]{1,0:T(8,128)}, f32[128,128]{1,0:T(8,128)}) custom-call(f32[128,128]{1,0:T(8,128)S(1)} %get-tuple-element.4.s_ref, f32[128,128]{1,0:T(8,128)S(1)} %get-tuple-element.5.r_ref), custom_call_target="tpu_custom_call" | custom-call | tf_op jit(solution)/shard_map/store/pallas_call | solution.py:397

commit v4 on v3

--- a/solution.py
+++ b/solution.py
@@ -114,7 +114,7 @@
     gi_here = pltpu.make_async_copy(g_own, gi.at[mine], local_sem.at[0])
     gj_here = pltpu.make_async_copy(g_own, gj.at[mine], local_sem.at[2])
 
-    for r in range(1, 8):
+    for r in (4, 3, 5, 2, 6, 1, 7):
         remote(g_own, gj.at[mine], g_send, gj_recv, at(step(z, r, 8), kx, ky, c)).start()
 
     @pl.when(i != tj)
@@ -125,7 +125,7 @@
     def _():
         gj_here.start()
 
-    for r in range(N):
+    for r in (10, 2, 8, 6, 14, 9, 11, 5, 7, 13, 15, 1, 3, 4, 12, 0):
         sx, sy = r % 4, r // 4
         if r:
             remote(
@@ -234,20 +234,27 @@
         between()
 
         half = row.at[0, pl.ds(0, HALF)]
-        for s in STEPS:
+        def relay_xy(s):
             row_wait(("x", s), half)
-            for t in STEPS:
+            for t in (2, 1, 3):
                 row_send("rest", from_xy(s, 0), 0, y_to(t))
             row_wait(("y", s), half)
-            for t in STEPS:
+            for t in (2, 1, 3):
                 row_send("rest", from_xy(0, s), 1, x_to(t))
-        for h in (0, 1):
+
+        def relay_z(h):
             for d in (0, 1):
                 slot = from_z(away[d], c)
                 col_wait(("z", 2, d, h), half)
                 if h == d:
                     col_send(("z", 4), slot, h, z_to(away[d]))
                 col_send(("z", 3, d), slot, h, z_to(near[d]))
+
+        relay_xy(STEPS[0])
+        relay_xy(STEPS[1])
+        relay_z(0)
+        relay_xy(STEPS[2])
+        relay_z(1)
         for d in (0, 1):
             col_send("near", from_z(away[d], c), None, other)
         col_wait(("z", 1), col.at[pl.ds(0, 2)])
@@ -260,20 +267,16 @@
         col_send("far", from_z(4, c), None, other)
         row_wait("rest", row.at[pl.ds(0, 12)])
         col_wait("near", col.at[pl.ds(0, 5)])
-        total = product(step(z, 0, 8))
-        for dz in (1, 7, 2, 6):
-            total = total + product(step(z, dz, 8))
+        total = product([step(z, dz, 8) for dz in (0, 1, 7, 2, 6)])
         col_wait("far", col.at[pl.ds(0, 3)])
-        for dz in (3, 5, 4):
-            total = total + product(step(z, dz, 8))
-        return total
+        return total + product([step(z, dz, 8) for dz in (3, 5, 4)])
 
     row1[tj] = stat
     col1[ti] = stat
     s_swap = remote(row1.at[tj], s_far, swap_send.at[1], swap_recv.at[1], (ti, tj))
 
-    def pair(ref, k, axis):
-        return jnp.concatenate([ref[2 * k], ref[2 * k + 1]], axis=axis)
+    def tiles(ref, pairs, axis):
+        return jnp.concatenate([ref[2 * k + h] for k in pairs for h in (0, 1)], axis=axis)
 
     def keep_stat():
         s_out[...] = stat
@@ -282,8 +285,8 @@
         def _():
             s_swap.start()
 
-    def square(k):
-        return dot3(pair(row1, k, 1), pair(col1, k, 0))
+    def square(pairs):
+        return dot3(tiles(row1, pairs, 1), tiles(col1, pairs, 0))
 
     power = gather(
         row1, col1, c_send.at[0], c1_recv, r_send.at[0], r1_recv, keep_stat, square
@@ -304,15 +307,17 @@
 
     scales = []
 
-    def last(k):
+    def last(pairs):
         if not scales:
             bytes_of(norms.at[pl.ds(0, N - 1)], n_recv)
             total = jnp.sum(jnp.sum(norms[...], axis=0), axis=1, keepdims=True)
             inv = 1.0 / (2.0 * jnp.sqrt(total * (1.0 / (N * B))))
             scales.extend((inv, inv * inv))
         inv, inv2 = scales
-        factor = (-0.5625 * inv2 * inv) * pair(col1, k, 0) + (0.0625 * inv2 * inv2) * pair(col2, k, 0)
-        return dot3(pair(row2, k, 1), factor)
+        factor = (-0.5625 * inv2 * inv) * tiles(col1, pairs, 0) + (
+            0.0625 * inv2 * inv2
+        ) * tiles(col2, pairs, 0)
+        return dot3(tiles(row2, pairs, 1), factor)
 
     result = gather(
         row2, col2, c_send.at[1], c2_recv, r_send.at[1], r2_recv, send_norms, last

time: 48 us -> 47.7 us (level)
  no operation moved by 1% of the time
where the time goes in v4:
time: 47.7 us; the launch traced here: 47.5 us
  Pallas kernels  46.9 us (98%)
  between operations  0.64 us (1%)
    pallas_call x1, Pallas kernels, local(): pl.pallas_call(kernel, out_shape=(block, block), in_specs=[pl.BlockSpec(m...  46.2 us

profile of v4, /device:TPU:1, one launch (start us, length us, event | category | flops | bytes accessed | tf_op | source)
XLA Modules:
  0.0 47.5 jit_solution(6181334228844370564)
XLA Ops:
  0.6 46.2 %shampoo.1 = (f32[128,128]{1,0:T(8,128)S(1)}, f32[128,128]{1,0:T(8,128)S(1)}) custom-call(f32[32,128]{1,0:T(8,128)} %bitcast.1, f32[128,128]{1,0:T(8,128)} %o_hbm.1), custom_call_target="tpu_custom_call" | custom-call | tf_op jit(solution)/shard_map/shampoo/pallas_call | solution.py:382
  46.9 0.7 %store.1 = (f32[128,128]{1,0:T(8,128)}, f32[128,128]{1,0:T(8,128)}) custom-call(f32[128,128]{1,0:T(8,128)S(1)} %get-tuple-element.4.s_ref, f32[128,128]{1,0:T(8,128)S(1)} %get-tuple-element.5.r_ref), custom_call_target="tpu_custom_call" | custom-call | tf_op jit(solution)/shard_map/store/pallas_call | solution.py:402

commit v5 on v4

--- a/solution.py
+++ b/solution.py
@@ -172,11 +172,12 @@
         bytes_of(gi.at[pl.ds(0, 15 * PIECE)], gi_recv)
         gi_here.wait()
 
+    rows_of = (((0,), (0,)), ((), ()))
+    outer = dot3(gi[mine_half, :], gj[mine_half, :], rows_of)
     remote(
         gj.at[other_half], gj.at[other_half], g_send, gc_recv, (i, j + 1 - 2 * c)
     ).wait_recv()
-
-    outer = dot3(gi[...], gj[...], (((0,), (0,)), ((), ())))
+    outer = outer + dot3(gi[other_half, :], gj[other_half, :], rows_of)
 
     @pl.when(swapped)
     def _():

time: 47.7 us -> 47.3 us (level)
  no operation moved by 1% of the time
where the time goes in v5:
time: 47.3 us; the launch traced here: 47.1 us
  Pallas kernels  46.5 us (98%)
  between operations  0.64 us (1%)
    pallas_call x1, Pallas kernels, local(): pl.pallas_call(kernel, out_shape=(block, block), in_specs=[pl.BlockSpec(m...  45.8 us

profile of v5, /device:TPU:1, one launch (start us, length us, event | category | flops | bytes accessed | tf_op | source)
XLA Modules:
  0.0 47.1 jit_solution(12646441762020545307)
XLA Ops:
  0.6 45.8 %shampoo.1 = (f32[128,128]{1,0:T(8,128)S(1)}, f32[128,128]{1,0:T(8,128)S(1)}) custom-call(f32[32,128]{1,0:T(8,128)} %bitcast.1, f32[128,128]{1,0:T(8,128)} %o_hbm.1), custom_call_target="tpu_custom_call" | custom-call | tf_op jit(solution)/shard_map/shampoo/pallas_call | solution.py:383
  46.5 0.7 %store.1 = (f32[128,128]{1,0:T(8,128)}, f32[128,128]{1,0:T(8,128)}) custom-call(f32[128,128]{1,0:T(8,128)S(1)} %get-tuple-element.4.s_ref, f32[128,128]{1,0:T(8,128)S(1)} %get-tuple-element.5.r_ref), custom_call_target="tpu_custom_call" | custom-call | tf_op jit(solution)/shard_map/store/pallas_call | solution.py:403

commit v6 on v5

--- a/solution.py
+++ b/solution.py
@@ -268,16 +268,19 @@
         col_send("far", from_z(4, c), None, other)
         row_wait("rest", row.at[pl.ds(0, 12)])
         col_wait("near", col.at[pl.ds(0, 5)])
-        total = product([step(z, dz, 8) for dz in (0, 1, 7, 2, 6)])
+        total = product(
+            [from_z(dz, core) for dz in (0, 1, 7, 2, 6) for core in (c, 1 - c)]
+            + [from_z(dz, c) for dz in (3, 5, 4)]
+        )
         col_wait("far", col.at[pl.ds(0, 3)])
-        return total + product([step(z, dz, 8) for dz in (3, 5, 4)])
+        return total + product([from_z(dz, 1 - c) for dz in (3, 5, 4)])
 
     row1[tj] = stat
     col1[ti] = stat
     s_swap = remote(row1.at[tj], s_far, swap_send.at[1], swap_recv.at[1], (ti, tj))
 
-    def tiles(ref, pairs, axis):
-        return jnp.concatenate([ref[2 * k + h] for k in pairs for h in (0, 1)], axis=axis)
+    def tiles(ref, slots, axis):
+        return jnp.concatenate([ref[slot] for slot in slots], axis=axis)
 
     def keep_stat():
         s_out[...] = stat
@@ -286,8 +289,8 @@
         def _():
             s_swap.start()
 
-    def square(pairs):
-        return dot3(tiles(row1, pairs, 1), tiles(col1, pairs, 0))
+    def square(slots):
+        return dot3(tiles(row1, slots, 1), tiles(col1, slots, 0))
 
     power = gather(
         row1, col1, c_send.at[0], c1_recv, r_send.at[0], r1_recv, keep_stat, square
@@ -308,17 +311,17 @@
 
     scales = []
 
-    def last(pairs):
+    def last(slots):
         if not scales:
             bytes_of(norms.at[pl.ds(0, N - 1)], n_recv)
             total = jnp.sum(jnp.sum(norms[...], axis=0), axis=1, keepdims=True)
             inv = 1.0 / (2.0 * jnp.sqrt(total * (1.0 / (N * B))))
             scales.extend((inv, inv * inv))
         inv, inv2 = scales
-        factor = (-0.5625 * inv2 * inv) * tiles(col1, pairs, 0) + (
+        factor = (-0.5625 * inv2 * inv) * tiles(col1, slots, 0) + (
             0.0625 * inv2 * inv2
-        ) * tiles(col2, pairs, 0)
-        return dot3(tiles(row2, pairs, 1), factor)
+        ) * tiles(col2, slots, 0)
+        return dot3(tiles(row2, slots, 1), factor)
 
     result = gather(
         row2, col2, c_send.at[1], c2_recv, r_send.at[1], r2_recv, send_norms, last

time: 47.3 us -> 47.2 us (level)
  no operation moved by 1% of the time
where the time goes in v6:
time: 47.2 us; the launch traced here: 47 us
  Pallas kernels  46.4 us (98%)
  between operations  0.64 us (1%)
    pallas_call x1, Pallas kernels, local(): pl.pallas_call(kernel, out_shape=(block, block), in_specs=[pl.BlockSpec(m...  45.7 us

profile of v6, /device:TPU:1, one launch (start us, length us, event | category | flops | bytes accessed | tf_op | source)
XLA Modules:
  0.0 47.0 jit_solution(7401358862376042674)
XLA Ops:
  0.6 45.7 %shampoo.1 = (f32[128,128]{1,0:T(8,128)S(1)}, f32[128,128]{1,0:T(8,128)S(1)}) custom-call(f32[32,128]{1,0:T(8,128)} %bitcast.1, f32[128,128]{1,0:T(8,128)} %o_hbm.1), custom_call_target="tpu_custom_call" | custom-call | tf_op jit(solution)/shard_map/shampoo/pallas_call | solution.py:386
  46.3 0.7 %store.1 = (f32[128,128]{1,0:T(8,128)}, f32[128,128]{1,0:T(8,128)}) custom-call(f32[128,128]{1,0:T(8,128)S(1)} %get-tuple-element.4.s_ref, f32[128,128]{1,0:T(8,128)S(1)} %get-tuple-element.5.r_ref), custom_call_target="tpu_custom_call" | custom-call | tf_op jit(solution)/shard_map/store/pallas_call | solution.py:406

commit v7 on v6

--- a/solution.py
+++ b/solution.py
@@ -187,7 +187,7 @@
 
     stat = 0.9 * o_own[...] + outer * (1.0 / (N * PIECE))
 
-    def gather(row, col, c_send, c_recv, r_send, r_recv, between, product):
+    def gather(row, col, c_send, c_recv, r_send, r_recv, between, prepare, product):
         def row_send(key, slot, h, to):
             part = row.at[slot, pl.ds(h * HALF, HALF)]
             remote(part, part, r_send, r_recv.at[ROW_AT[key]], to).start()
@@ -266,6 +266,7 @@
             col_send("far", from_z((away[d] + near[d]) % 8, c), None, other)
         col_wait(("z", 4), col.at[0])
         col_send("far", from_z(4, c), None, other)
+        prepare()
         row_wait("rest", row.at[pl.ds(0, 12)])
         col_wait("near", col.at[pl.ds(0, 5)])
         total = product(
@@ -293,7 +294,7 @@
         return dot3(tiles(row1, slots, 1), tiles(col1, slots, 0))
 
     power = gather(
-        row1, col1, c_send.at[0], c1_recv, r_send.at[0], r1_recv, keep_stat, square
+        row1, col1, c_send.at[0], c1_recv, r_send.at[0], r1_recv, keep_stat, lambda: None, square
     )
     row2[tj] = power
     col2[ti] = power
@@ -311,12 +312,13 @@
 
     scales = []
 
+    def scale():
+        bytes_of(norms.at[pl.ds(0, N - 1)], n_recv)
+        total = jnp.sum(jnp.sum(norms[...], axis=0), axis=1, keepdims=True)
+        inv = 1.0 / (2.0 * jnp.sqrt(total * (1.0 / (N * B))))
+        scales.extend((inv, inv * inv))
+
     def last(slots):
-        if not scales:
-            bytes_of(norms.at[pl.ds(0, N - 1)], n_recv)
-            total = jnp.sum(jnp.sum(norms[...], axis=0), axis=1, keepdims=True)
-            inv = 1.0 / (2.0 * jnp.sqrt(total * (1.0 / (N * B))))
-            scales.extend((inv, inv * inv))
         inv, inv2 = scales
         factor = (-0.5625 * inv2 * inv) * tiles(col1, slots, 0) + (
             0.0625 * inv2 * inv2
@@ -324,7 +326,7 @@
         return dot3(tiles(row2, slots, 1), factor)
 
     result = gather(
-        row2, col2, c_send.at[1], c2_recv, r_send.at[1], r2_recv, send_norms, last
+        row2, col2, c_send.at[1], c2_recv, r_send.at[1], r2_recv, send_norms, scale, last
     )
     inv, inv2 = scales
     rows = lax.broadcasted_iota(jnp.int32, (B, B), 0)

time: 47.2 us -> 47.1 us (level)
  no operation moved by 1% of the time
where the time goes in v7:
time: 47.1 us; the launch traced here: 46.9 us
  Pallas kernels  46.3 us (98%)
  between operations  0.64 us (1%)
    pallas_call x1, Pallas kernels, local(): pl.pallas_call(kernel, out_shape=(block, block), in_specs=[pl.BlockSpec(m...  45.6 us

profile of v7, /device:TPU:1, one launch (start us, length us, event | category | flops | bytes accessed | tf_op | source)
XLA Modules:
  0.0 46.9 jit_solution(7570899377295930568)
XLA Ops:
  0.6 45.6 %shampoo.1 = (f32[128,128]{1,0:T(8,128)S(1)}, f32[128,128]{1,0:T(8,128)S(1)}) custom-call(f32[32,128]{1,0:T(8,128)} %bitcast.1, f32[128,128]{1,0:T(8,128)} %o_hbm.1), custom_call_target="tpu_custom_call" | custom-call | tf_op jit(solution)/shard_map/shampoo/pallas_call | solution.py:388
  46.3 0.7 %store.1 = (f32[128,128]{1,0:T(8,128)}, f32[128,128]{1,0:T(8,128)}) custom-call(f32[128,128]{1,0:T(8,128)S(1)} %get-tuple-element.4.s_ref, f32[128,128]{1,0:T(8,128)S(1)} %get-tuple-element.5.r_ref), custom_call_target="tpu_custom_call" | custom-call | tf_op jit(solution)/shard_map/store/pallas_call | solution.py:408

commit v8 on v7

--- a/solution.py
+++ b/solution.py
@@ -93,7 +93,6 @@
     @pl.when(swapped)
     def _():
         greet((ti, j))
-        greet((ti, tj))
 
     for s in STEPS:
         greet(at(z, step(x, s, 4), y, c))
@@ -104,7 +103,7 @@
         greet(at(step(z, s, 8), x, y, 1 - c))
     g_in.wait()
     same = 1 - (c - xl) * (c - xl)
-    pl.semaphore_wait(barrier, 46 - 2 * same - (i == tj).astype(jnp.int32))
+    pl.semaphore_wait(barrier, 45 - same - (i == tj).astype(jnp.int32))
 
     order = lax.rem(j, 2) * 8 + lax.div(j, 2)
     mine = pl.ds(pl.multiple_of(order * PIECE, PIECE), PIECE)

time: 47.1 us -> 47.1 us (level)
  no operation moved by 1% of the time
where the time goes in v8:
time: 47.1 us; the launch traced here: 47 us
  Pallas kernels  46.3 us (98%)
  between operations  0.64 us (1%)
    pallas_call x1, Pallas kernels, local(): pl.pallas_call(kernel, out_shape=(block, block), in_specs=[pl.BlockSpec(m...  45.7 us

profile of v8, /device:TPU:1, one launch (start us, length us, event | category | flops | bytes accessed | tf_op | source)
XLA Modules:
  0.0 47.0 jit_solution(532082580807464235)
XLA Ops:
  0.6 45.7 %shampoo.1 = (f32[128,128]{1,0:T(8,128)S(1)}, f32[128,128]{1,0:T(8,128)S(1)}) custom-call(f32[32,128]{1,0:T(8,128)} %bitcast.1, f32[128,128]{1,0:T(8,128)} %o_hbm.1), custom_call_target="tpu_custom_call" | custom-call | tf_op jit(solution)/shard_map/shampoo/pallas_call | solution.py:387
  46.3 0.7 %store.1 = (f32[128,128]{1,0:T(8,128)}, f32[128,128]{1,0:T(8,128)}) custom-call(f32[128,128]{1,0:T(8,128)S(1)} %get-tuple-element.4.s_ref, f32[128,128]{1,0:T(8,128)S(1)} %get-tuple-element.5.r_ref), custom_call_target="tpu_custom_call" | custom-call | tf_op jit(solution)/shard_map/store/pallas_call | solution.py:407
